TPU v7x, 32 devices: a whole 2x2x4 slice. The times are simulated.
32 devices in a mesh: sfc: 32 (over z, y, x, core).
Axes of the slice: x: 2, y: 2, z: 4, core: 2. Of those that a mesh axis runs over, the one named last changes fastest.
Arguments:
- tracers: float32 [2048, 3, 480], P('sfc'), may hold values from -6 to 6
- weights: float32 [2, 2048, 3, 256], P(None, 'sfc'), may hold values from -1.5 to 1.5
- departure: int32 [2048, 48], P('sfc'), may hold values from 0 to 95, as said below
- needs: int32 [32, 8, 4], P('sfc'), may hold values from 0 to 63
- counts: int32 [32, 8], P('sfc'), may hold values from 1 to 4, as said below
Outputs:
- mixed: float32 [2048, 3, 480], P('sfc')
Inputs may be any that keep to these rules, and one draw needn't show every extreme that they name: `departure`: each entry is a slot of its range's source table: below 64 a local element; otherwise 64 + j * 4 + c with c below counts[r, j] of its range r. `counts`: some range uses all 4 entries of every list in every draw.
All inputs are finite; a program needn't handle non-finite values.
Results may differ from a plain program's by a relative error of at most 0.0003.
Values sent between devices are 32-bit elements; how exact they have to be, the bound alone decides.
A program may use at most 64 MiB of HBM per device.

v0:
```python
import math

import jax
import jax.numpy as jnp
from jax import lax
from jax.sharding import PartitionSpec as P

NODES = 16
TRACERS = 30
LEV = 3
SUBSTEPS = 2
REACH = 4
CAP = 4


def passed_along(value, axis, steps):
    count = lax.axis_size(axis)
    pairs = [(source, (source + steps) % count) for source in range(count)]
    return lax.ppermute(value, axis, pairs)


def interpolate(source_table, dep_block, weight_block):
    elements = dep_block.shape[0]
    block_rows = math.gcd(elements, 32)
    flat_rows = source_table.reshape(-1, NODES * TRACERS)
    slot_rows = (
        dep_block.reshape(elements, LEV, NODES) * LEV
        + jnp.arange(LEV, dtype=jnp.int32)[None, :, None]
    )

    def per_block(inputs):
        row_index, matrices = inputs
        gathered = flat_rows[row_index].reshape(block_rows, LEV, NODES, NODES, TRACERS)
        matrices = matrices.reshape(block_rows, LEV, NODES, NODES)
        values = jnp.einsum("elts,eltsq->eltq", matrices, gathered, precision=lax.Precision.HIGHEST)
        lowest = jnp.min(gathered, axis=3)
        highest = jnp.max(gathered, axis=3)
        return jnp.clip(values, lowest, highest).reshape(block_rows, LEV, NODES * TRACERS)

    result = lax.map(
        per_block,
        (
            slot_rows.reshape(elements // block_rows, block_rows, LEV, NODES),
            weight_block.reshape(elements // block_rows, block_rows, LEV, NODES * NODES),
        ),
    )
    return result.reshape(elements, LEV, NODES * TRACERS)


def on_device(tracers, weights, departure, needs, counts):
    offsets = [slot - REACH if slot < REACH else slot - REACH + 1 for slot in range(2 * REACH)]
    live_slots = (jnp.arange(CAP, dtype=jnp.int32)[None, :] < counts[0][:, None])[:, :, None, None]
    wanted = needs[0]
    asked_lists = [passed_along(wanted[slot], "sfc", offsets[slot]) for slot in range(2 * REACH)]
    current = tracers
    for substep in range(SUBSTEPS):
        pieces = []
        for slot in range(2 * REACH):
            pieces.append(passed_along(current[asked_lists[slot]], "sfc", -offsets[slot]))
        fetched = jnp.where(live_slots, jnp.stack(pieces), 0.0)
        source_table = jnp.concatenate(
            [current, fetched.reshape(2 * REACH * CAP, LEV, NODES * TRACERS)], axis=0
        )
        current = interpolate(source_table, departure, weights[substep])
    return current


def solution(mesh):
    return jax.shard_map(
        on_device,
        mesh=mesh,
        in_specs=(
            P("sfc", None, None),
            P(None, "sfc", None, None),
            P("sfc", None),
            P("sfc", None, None),
            P("sfc", None),
        ),
        out_specs=P("sfc", None, None),
        check_vma=False,
    )
```

profile of v0, /device:TPU:0, one launch (start us, length us, event | category | flops | bytes accessed | tf_op | source)
XLA Modules:
  0.0 231.7 jit_solution(12130063704361718443)
XLA Ops:
  1.3 5.5 %collective-permute-start.2 = (s32[4]{0:T(128)S(1)}, s32[4]{0:T(128)S(1)}, u32[]{:S(2)}, u32[]{:S(2)}) collective-permute-start(s32[4]{0:T(128)S(1)} %get-tuple-element.110), channel_id=1, source_target_pairs={{0,29},{1,30},{2,31},{3,0},{4,1},{5,2},{6,3},{7,4},{8,5},{9,6},{10... | collective-permute-start | bytes 56 | tf_op jit(solution)/shard_map/ppermute | solution.py:19
  18.6 2.7 %collective-permute-start.12 = (s32[4]{0:T(128)S(1)}, s32[4]{0:T(128)S(1)}, u32[]{:S(2)}, u32[]{:S(2)}) collective-permute-start(s32[4]{0:T(128)S(1)} %get-tuple-element.112), channel_id=1, source_target_pairs={{0,3},{1,4},{2,5},{3,6},{4,7},{5,8},{6,9},{7,10},{8,11},{9,12},{10... | collective-permute-start | bytes 56 | tf_op jit(solution)/shard_map/ppermute | solution.py:19
  28.2 5.3 %collective-permute-start.9 = (f32[4,3,480]{2,0,1:T(4,128)S(1)}, f32[4,3,480]{2,0,1:T(4,128)S(1)}, u32[]{:S(2)}, u32[]{:S(2)}) collective-permute-start(f32[4,3,480]{2,0,1:T(4,128)S(1)} %gather_fusion.6), channel_id=1, source_target_pairs={{0,31},{1,0},{2,1},{3,2},{4,3},{5,4},{6,5},{7,6},{8,7},{9,8},{10,9... | collective-permute-start | bytes 69128 | tf_op jit(solution)/shard_map/ppermute | solution.py:19
  40.2 2.7 %collective-permute-start.15 = (f32[4,3,480]{2,0,1:T(4,128)S(1)}, f32[4,3,480]{2,0,1:T(4,128)S(1)}, u32[]{:S(2)}, u32[]{:S(2)}) collective-permute-start(f32[4,3,480]{2,0,1:T(4,128)S(1)} %gather_fusion.9), channel_id=1, source_target_pairs={{0,28},{1,29},{2,30},{3,31},{4,0},{5,1},{6,2},{7,3},{8,4},{9,5},{1... | collective-permute-start | bytes 69128 | tf_op jit(solution)/shard_map/ppermute | solution.py:19
  46.4 82.4 %while.20 = (s32[]{:T(128)}, f32[2,32,3,480]{3,1,0,2:T(8,128)S(1)}, s32[2,32,3,16]{3,2,1,0:T(4,128)S(1)}, f32[288,480]{1,0:T(8,128)S(1)}, f32[2,32,3,256]{3,1,0,2:T(8,128)S(1)}, /*index=5*/s32[]{:T(128)}) while((s32[]{:T(128)}, f32[2,32,3,480]{3,1,0,2:T(8,128)S(1)}, s32[2,32,3,16]{3,2,1,0:T(4,128)S(1)}, f32[288,480]{1,0:T(8,128)S(1)}, ...), condition=%wide.region_3.4_spmd, body=%wide.region_0.3_spmd.sunk | while | flops 10328578 | bytes 20545616 | solution.py:40
  46.7 5.0 %gather_fusion = f32[1536,480]{1,0:T(8,128)} fusion(f32[288,480]{1,0:T(8,128)S(1)} %get-tuple-element.228, s32[2048]{0:T(1024)S(1)} %pad_clamp_fusion.12), kind=kCustom, calls=%fused_computation.clone.1 | custom fusion | bytes 5904384 | tf_op jit(solution)/shard_map/while/body/eval_jaxpr/gather | solution.py:33
  51.7 10.8 %reshape.332 = f32[32,3,16,16,30]{4,3,2,1,0:T(8,128)} reshape(f32[1536,480]{1,0:T(8,128)} %gather_fusion) | data formatting | bytes 5898240 | tf_op jit(solution)/shard_map/while/body/eval_jaxpr/reshape | solution.py:33
  63.3 13.3 %fusion.20 = f32[32,3,16,1,30]{4,3,2,1,0:T(1,128)S(1)} fusion(f32[32,3,16,16,1]{3,4,2,1,0:T(1,128)S(1)} %copy.92, f32[32,3,16,16,30]{4,3,2,1,0:T(8,128)} %reshape.332), kind=kOutput, calls=%fused_computation.78.clone.1 | convolution fusion | flops 8847360 | bytes 3231744 | tf_op jit(solution)/shard_map/while/body/eval_jaxpr/elts,eltsq->eltq/dot_general | solution.py:35
  76.6 10.2 %fusion.19 = (f32[32,3,16,30]{3,2,1,0:T(8,128)S(1)}, f32[32,3,16,30]{3,2,1,0:T(8,128)S(1)}) fusion(f32[32,3,16,16,30]{4,3,2,1,0:T(8,128)} %reshape.332), kind=kLoop, calls=%fused_computation.75.clone.1 | loop fusion | flops 1382400 | bytes 3317760 | tf_op jit(solution)/shard_map/while/body/eval_jaxpr/reduce_min | solution.py:36
  87.8 5.0 %gather_fusion = f32[1536,480]{1,0:T(8,128)} fusion(f32[288,480]{1,0:T(8,128)S(1)} %get-tuple-element.228, s32[2048]{0:T(1024)S(1)} %pad_clamp_fusion.12), kind=kCustom, calls=%fused_computation.clone.1 | custom fusion | bytes 5904384 | tf_op jit(solution)/shard_map/while/body/eval_jaxpr/gather | solution.py:33
  92.8 10.8 %reshape.332 = f32[32,3,16,16,30]{4,3,2,1,0:T(8,128)} reshape(f32[1536,480]{1,0:T(8,128)} %gather_fusion) | data formatting | bytes 5898240 | tf_op jit(solution)/shard_map/while/body/eval_jaxpr/reshape | solution.py:33
  104.4 13.3 %fusion.20 = f32[32,3,16,1,30]{4,3,2,1,0:T(1,128)S(1)} fusion(f32[32,3,16,16,1]{3,4,2,1,0:T(1,128)S(1)} %copy.92, f32[32,3,16,16,30]{4,3,2,1,0:T(8,128)} %reshape.332), kind=kOutput, calls=%fused_computation.78.clone.1 | convolution fusion | flops 8847360 | bytes 3231744 | tf_op jit(solution)/shard_map/while/body/eval_jaxpr/elts,eltsq->eltq/dot_general | solution.py:35
  117.7 10.2 %fusion.19 = (f32[32,3,16,30]{3,2,1,0:T(8,128)S(1)}, f32[32,3,16,30]{3,2,1,0:T(8,128)S(1)}) fusion(f32[32,3,16,16,30]{4,3,2,1,0:T(8,128)} %reshape.332), kind=kLoop, calls=%fused_computation.75.clone.1 | loop fusion | flops 1382400 | bytes 3317760 | tf_op jit(solution)/shard_map/while/body/eval_jaxpr/reduce_min | solution.py:36
  136.1 5.3 %collective-permute-start.20 = (f32[4,3,480]{2,1,0:T(4,128)S(1)}, f32[4,3,480]{2,1,0:T(4,128)S(1)}, u32[]{:S(2)}, u32[]{:S(2)}) collective-permute-start(f32[4,3,480]{2,1,0:T(4,128)S(1)} %gather_fusion.14), channel_id=1, source_target_pairs={{0,31},{1,0},{2,1},{3,2},{4,3},{5,4},{6,5},{7,6},{8,7},{9,8},{10,9... | collective-permute-start | bytes 69128 | tf_op jit(solution)/shard_map/ppermute | solution.py:19
  143.3 2.7 %collective-permute-start.23 = (f32[4,3,480]{2,1,0:T(4,128)S(1)}, f32[4,3,480]{2,1,0:T(4,128)S(1)}, u32[]{:S(2)}, u32[]{:S(2)}) collective-permute-start(f32[4,3,480]{2,1,0:T(4,128)S(1)} %gather_fusion.17), channel_id=1, source_target_pairs={{0,28},{1,29},{2,30},{3,31},{4,0},{5,1},{6,2},{7,3},{8,4},{9,5},{1... | collective-permute-start | bytes 69128 | tf_op jit(solution)/shard_map/ppermute | solution.py:19
  148.5 82.4 %while.21 = (s32[]{:T(128)}, f32[2,32,3,480]{3,1,0,2:T(8,128)S(1)}, s32[2,32,3,16]{3,2,1,0:T(4,128)S(1)}, f32[288,480]{1,0:T(8,128)S(1)}, f32[2,32,3,256]{3,1,0,2:T(8,128)S(1)}, /*index=5*/s32[]{:T(128)}) while((s32[]{:T(128)}, f32[2,32,3,480]{3,1,0,2:T(8,128)S(1)}, s32[2,32,3,16]{3,2,1,0:T(4,128)S(1)}, f32[288,480]{1,0:T(8,128)S(1)}, ...), condition=%wide.region_7.8_spmd, body=%wide.region_4.7_spmd.sunk | while | flops 10328578 | bytes 20545616 | solution.py:40
  148.9 5.0 %gather_fusion.1 = f32[1536,480]{1,0:T(8,128)} fusion(f32[288,480]{1,0:T(8,128)S(1)} %get-tuple-element.246, s32[2048]{0:T(1024)S(1)} %pad_clamp_fusion.13), kind=kCustom, calls=%fused_computation.1.clone.1 | custom fusion | bytes 5904384 | tf_op jit(solution)/shard_map/while/body/eval_jaxpr/gather | solution.py:33
  153.8 10.8 %reshape.337 = f32[32,3,16,16,30]{4,3,2,1,0:T(8,128)} reshape(f32[1536,480]{1,0:T(8,128)} %gather_fusion.1) | data formatting | bytes 5898240 | tf_op jit(solution)/shard_map/while/body/eval_jaxpr/reshape | solution.py:33
  165.5 13.3 %fusion.24 = f32[32,3,16,1,30]{4,3,2,1,0:T(1,128)S(1)} fusion(f32[32,3,16,16,1]{3,4,2,1,0:T(1,128)S(1)} %copy.95, f32[32,3,16,16,30]{4,3,2,1,0:T(8,128)} %reshape.337), kind=kOutput, calls=%fused_computation.79.clone.1 | convolution fusion | flops 8847360 | bytes 3231744 | tf_op jit(solution)/shard_map/while/body/eval_jaxpr/elts,eltsq->eltq/dot_general | solution.py:35
  178.8 10.2 %fusion.23 = (f32[32,3,16,30]{3,2,1,0:T(8,128)S(1)}, f32[32,3,16,30]{3,2,1,0:T(8,128)S(1)}) fusion(f32[32,3,16,16,30]{4,3,2,1,0:T(8,128)} %reshape.337), kind=kLoop, calls=%fused_computation.76.clone.1 | loop fusion | flops 1382400 | bytes 3317760 | tf_op jit(solution)/shard_map/while/body/eval_jaxpr/reduce_min | solution.py:36
  190.0 5.0 %gather_fusion.1 = f32[1536,480]{1,0:T(8,128)} fusion(f32[288,480]{1,0:T(8,128)S(1)} %get-tuple-element.246, s32[2048]{0:T(1024)S(1)} %pad_clamp_fusion.13), kind=kCustom, calls=%fused_computation.1.clone.1 | custom fusion | bytes 5904384 | tf_op jit(solution)/shard_map/while/body/eval_jaxpr/gather | solution.py:33
  194.9 10.8 %reshape.337 = f32[32,3,16,16,30]{4,3,2,1,0:T(8,128)} reshape(f32[1536,480]{1,0:T(8,128)} %gather_fusion.1) | data formatting | bytes 5898240 | tf_op jit(solution)/shard_map/while/body/eval_jaxpr/reshape | solution.py:33
  206.5 13.3 %fusion.24 = f32[32,3,16,1,30]{4,3,2,1,0:T(1,128)S(1)} fusion(f32[32,3,16,16,1]{3,4,2,1,0:T(1,128)S(1)} %copy.95, f32[32,3,16,16,30]{4,3,2,1,0:T(8,128)} %reshape.337), kind=kOutput, calls=%fused_computation.79.clone.1 | convolution fusion | flops 8847360 | bytes 3231744 | tf_op jit(solution)/shard_map/while/body/eval_jaxpr/elts,eltsq->eltq/dot_general | solution.py:35
  219.9 10.2 %fusion.23 = (f32[32,3,16,30]{3,2,1,0:T(8,128)S(1)}, f32[32,3,16,30]{3,2,1,0:T(8,128)S(1)}) fusion(f32[32,3,16,16,30]{4,3,2,1,0:T(8,128)} %reshape.337), kind=kLoop, calls=%fused_computation.76.clone.1 | loop fusion | flops 1382400 | bytes 3317760 | tf_op jit(solution)/shard_map/while/body/eval_jaxpr/reduce_min | solution.py:36
  (145 shorter events, 49.1 us)
Async XLA Ops:
  1.3 12.7 %collective-permute-start.2 = (s32[4]{0:T(128)S(1)}, s32[4]{0:T(128)S(1)}, u32[]{:S(2)}, u32[]{:S(2)}) collective-permute-start(s32[4]{0:T(128)S(1)} %get-tuple-element.110), channel_id=1, source_target_pairs={{0,29},{1,30},{2,31},{3,0},{4,1},{5,2},{6,3},{7,4},{8,5},{9,6},{10... | collective-permute-start | bytes 56 | tf_op jit(solution)/shard_map/ppermute | solution.py:19
  6.8 7.3 %collective-permute-start = (s32[4]{0:T(128)S(1)}, s32[4]{0:T(128)S(1)}, u32[]{:S(2)}, u32[]{:S(2)}) collective-permute-start(s32[4]{0:T(128)S(1)} %get-tuple-element.111), channel_id=1, source_target_pairs={{0,28},{1,29},{2,30},{3,31},{4,0},{5,1},{6,2},{7,3},{8,4},{9,5},{1... | collective-permute-start | bytes 56 | tf_op jit(solution)/shard_map/ppermute | solution.py:19
  7.4 11.1 %collective-permute-start.6 = (s32[4]{0:T(128)S(1)}, s32[4]{0:T(128)S(1)}, u32[]{:S(2)}, u32[]{:S(2)}) collective-permute-start(s32[4]{0:T(128)S(1)} %get-tuple-element.108), channel_id=1, source_target_pairs={{0,31},{1,0},{2,1},{3,2},{4,3},{5,4},{6,5},{7,6},{8,7},{9,8},{10,9... | collective-permute-start | bytes 56 | tf_op jit(solution)/shard_map/ppermute | solution.py:19
  8.8 12.5 %collective-permute-start.4 = (s32[4]{0:T(128)S(1)}, s32[4]{0:T(128)S(1)}, u32[]{:S(2)}, u32[]{:S(2)}) collective-permute-start(s32[4]{0:T(128)S(1)} %get-tuple-element.109), channel_id=1, source_target_pairs={{0,30},{1,31},{2,0},{3,1},{4,2},{5,3},{6,4},{7,5},{8,6},{9,7},{10,... | collective-permute-start | bytes 56 | tf_op jit(solution)/shard_map/ppermute | solution.py:19
  11.1 13.7 %collective-permute-start.10 = (s32[4]{0:T(128)S(1)}, s32[4]{0:T(128)S(1)}, u32[]{:S(2)}, u32[]{:S(2)}) collective-permute-start(s32[4]{0:T(128)S(1)} %get-tuple-element.106), channel_id=1, source_target_pairs={{0,2},{1,3},{2,4},{3,5},{4,6},{5,7},{6,8},{7,9},{8,10},{9,11},{10,... | collective-permute-start | bytes 56 | tf_op jit(solution)/shard_map/ppermute | solution.py:19
  14.0 11.0 %collective-permute-start.8 = (s32[4]{0:T(128)S(1)}, s32[4]{0:T(128)S(1)}, u32[]{:S(2)}, u32[]{:S(2)}) collective-permute-start(s32[4]{0:T(128)S(1)} %get-tuple-element.107), channel_id=1, source_target_pairs={{0,1},{1,2},{2,3},{3,4},{4,5},{5,6},{6,7},{7,8},{8,9},{9,10},{10,1... | collective-permute-start | bytes 56 | tf_op jit(solution)/shard_map/ppermute | solution.py:19
  14.1 14.0 %collective-permute-start.14 = (s32[4]{0:T(128)S(1)}, s32[4]{0:T(128)S(1)}, u32[]{:S(2)}, u32[]{:S(2)}) collective-permute-start(s32[4]{0:T(128)S(1)} %get-tuple-element.105), channel_id=1, source_target_pairs={{0,4},{1,5},{2,6},{3,7},{4,8},{5,9},{6,10},{7,11},{8,12},{9,13},{1... | collective-permute-start | bytes 56 | tf_op jit(solution)/shard_map/ppermute | solution.py:19
  18.6 9.6 %collective-permute-start.12 = (s32[4]{0:T(128)S(1)}, s32[4]{0:T(128)S(1)}, u32[]{:S(2)}, u32[]{:S(2)}) collective-permute-start(s32[4]{0:T(128)S(1)} %get-tuple-element.112), channel_id=1, source_target_pairs={{0,3},{1,4},{2,5},{3,6},{4,7},{5,8},{6,9},{7,10},{8,11},{9,12},{10... | collective-permute-start | bytes 56 | tf_op jit(solution)/shard_map/ppermute | solution.py:19
  21.3 17.1 %collective-permute-start.1 = (f32[4,3,480]{2,0,1:T(4,128)S(1)}, f32[4,3,480]{2,0,1:T(4,128)S(1)}, u32[]{:S(2)}, u32[]{:S(2)}) collective-permute-start(f32[4,3,480]{2,0,1:T(4,128)S(1)} %gather_fusion.2), channel_id=1, source_target_pairs={{0,4},{1,5},{2,6},{3,7},{4,8},{5,9},{6,10},{7,11},{8,12},{9,13},{1... | collective-permute-start | bytes 69128 | tf_op jit(solution)/shard_map/ppermute | solution.py:19
  24.8 14.1 %collective-permute-start.3 = (f32[4,3,480]{2,0,1:T(4,128)S(1)}, f32[4,3,480]{2,0,1:T(4,128)S(1)}, u32[]{:S(2)}, u32[]{:S(2)}) collective-permute-start(f32[4,3,480]{2,0,1:T(4,128)S(1)} %gather_fusion.3), channel_id=1, source_target_pairs={{0,3},{1,4},{2,5},{3,6},{4,7},{5,8},{6,9},{7,10},{8,11},{9,12},{10... | collective-permute-start | bytes 69128 | tf_op jit(solution)/shard_map/ppermute | solution.py:19
  25.0 15.2 %collective-permute-start.5 = (f32[4,3,480]{2,0,1:T(4,128)S(1)}, f32[4,3,480]{2,0,1:T(4,128)S(1)}, u32[]{:S(2)}, u32[]{:S(2)}) collective-permute-start(f32[4,3,480]{2,0,1:T(4,128)S(1)} %gather_fusion.4), channel_id=1, source_target_pairs={{0,2},{1,3},{2,4},{3,5},{4,6},{5,7},{6,8},{7,9},{8,10},{9,11},{10,... | collective-permute-start | bytes 69128 | tf_op jit(solution)/shard_map/ppermute | solution.py:19
  28.1 14.8 %collective-permute-start.7 = (f32[4,3,480]{2,0,1:T(4,128)S(1)}, f32[4,3,480]{2,0,1:T(4,128)S(1)}, u32[]{:S(2)}, u32[]{:S(2)}) collective-permute-start(f32[4,3,480]{2,0,1:T(4,128)S(1)} %gather_fusion.5), channel_id=1, source_target_pairs={{0,1},{1,2},{2,3},{3,4},{4,5},{5,6},{6,7},{7,8},{8,9},{9,10},{10,1... | collective-permute-start | bytes 69128 | tf_op jit(solution)/shard_map/ppermute | solution.py:19
  28.2 14.7 %collective-permute-start.9 = (f32[4,3,480]{2,0,1:T(4,128)S(1)}, f32[4,3,480]{2,0,1:T(4,128)S(1)}, u32[]{:S(2)}, u32[]{:S(2)}) collective-permute-start(f32[4,3,480]{2,0,1:T(4,128)S(1)} %gather_fusion.6), channel_id=1, source_target_pairs={{0,31},{1,0},{2,1},{3,2},{4,3},{5,4},{6,5},{7,6},{8,7},{9,8},{10,9... | collective-permute-start | bytes 69128 | tf_op jit(solution)/shard_map/ppermute | solution.py:19
  38.4 4.5 %collective-permute-start.11 = (f32[4,3,480]{2,0,1:T(4,128)S(1)}, f32[4,3,480]{2,0,1:T(4,128)S(1)}, u32[]{:S(2)}, u32[]{:S(2)}) collective-permute-start(f32[4,3,480]{2,0,1:T(4,128)S(1)} %gather_fusion.7), channel_id=1, source_target_pairs={{0,30},{1,31},{2,0},{3,1},{4,2},{5,3},{6,4},{7,5},{8,6},{9,7},{10,... | collective-permute-start | bytes 69128 | tf_op jit(solution)/shard_map/ppermute | solution.py:19
  39.0 3.9 %collective-permute-start.13 = (f32[4,3,480]{2,0,1:T(4,128)S(1)}, f32[4,3,480]{2,0,1:T(4,128)S(1)}, u32[]{:S(2)}, u32[]{:S(2)}) collective-permute-start(f32[4,3,480]{2,0,1:T(4,128)S(1)} %gather_fusion.8), channel_id=1, source_target_pairs={{0,29},{1,30},{2,31},{3,0},{4,1},{5,2},{6,3},{7,4},{8,5},{9,6},{10... | collective-permute-start | bytes 69128 | tf_op jit(solution)/shard_map/ppermute | solution.py:19
  40.2 4.2 %collective-permute-start.15 = (f32[4,3,480]{2,0,1:T(4,128)S(1)}, f32[4,3,480]{2,0,1:T(4,128)S(1)}, u32[]{:S(2)}, u32[]{:S(2)}) collective-permute-start(f32[4,3,480]{2,0,1:T(4,128)S(1)} %gather_fusion.9), channel_id=1, source_target_pairs={{0,28},{1,29},{2,30},{3,31},{4,0},{5,1},{6,2},{7,3},{8,4},{9,5},{1... | collective-permute-start | bytes 69128 | tf_op jit(solution)/shard_map/ppermute | solution.py:19
  129.6 11.9 %collective-permute-start.16 = (f32[4,3,480]{2,1,0:T(4,128)S(1)}, f32[4,3,480]{2,1,0:T(4,128)S(1)}, u32[]{:S(2)}, u32[]{:S(2)}) collective-permute-start(f32[4,3,480]{2,1,0:T(4,128)S(1)} %gather_fusion.10), channel_id=1, source_target_pairs={{0,4},{1,5},{2,6},{3,7},{4,8},{5,9},{6,10},{7,11},{8,12},{9,13},{1... | collective-permute-start | bytes 69128 | tf_op jit(solution)/shard_map/ppermute | solution.py:19
  134.3 7.5 %collective-permute-start.17 = (f32[4,3,480]{2,1,0:T(4,128)S(1)}, f32[4,3,480]{2,1,0:T(4,128)S(1)}, u32[]{:S(2)}, u32[]{:S(2)}) collective-permute-start(f32[4,3,480]{2,1,0:T(4,128)S(1)} %gather_fusion.11), channel_id=1, source_target_pairs={{0,3},{1,4},{2,5},{3,6},{4,7},{5,8},{6,9},{7,10},{8,11},{9,12},{10... | collective-permute-start | bytes 69128 | tf_op jit(solution)/shard_map/ppermute | solution.py:19
  134.4 8.9 %collective-permute-start.18 = (f32[4,3,480]{2,1,0:T(4,128)S(1)}, f32[4,3,480]{2,1,0:T(4,128)S(1)}, u32[]{:S(2)}, u32[]{:S(2)}) collective-permute-start(f32[4,3,480]{2,1,0:T(4,128)S(1)} %gather_fusion.12), channel_id=1, source_target_pairs={{0,2},{1,3},{2,4},{3,5},{4,6},{5,7},{6,8},{7,9},{8,10},{9,11},{10,... | collective-permute-start | bytes 69128 | tf_op jit(solution)/shard_map/ppermute | solution.py:19
  136.1 9.9 %collective-permute-start.19 = (f32[4,3,480]{2,1,0:T(4,128)S(1)}, f32[4,3,480]{2,1,0:T(4,128)S(1)}, u32[]{:S(2)}, u32[]{:S(2)}) collective-permute-start(f32[4,3,480]{2,1,0:T(4,128)S(1)} %gather_fusion.13), channel_id=1, source_target_pairs={{0,1},{1,2},{2,3},{3,4},{4,5},{5,6},{6,7},{7,8},{8,9},{9,10},{10,1... | collective-permute-start | bytes 69128 | tf_op jit(solution)/shard_map/ppermute | solution.py:19
  136.1 9.9 %collective-permute-start.20 = (f32[4,3,480]{2,1,0:T(4,128)S(1)}, f32[4,3,480]{2,1,0:T(4,128)S(1)}, u32[]{:S(2)}, u32[]{:S(2)}) collective-permute-start(f32[4,3,480]{2,1,0:T(4,128)S(1)} %gather_fusion.14), channel_id=1, source_target_pairs={{0,31},{1,0},{2,1},{3,2},{4,3},{5,4},{6,5},{7,6},{8,7},{9,8},{10,9... | collective-permute-start | bytes 69128 | tf_op jit(solution)/shard_map/ppermute | solution.py:19
  141.5 4.6 %collective-permute-start.21 = (f32[4,3,480]{2,1,0:T(4,128)S(1)}, f32[4,3,480]{2,1,0:T(4,128)S(1)}, u32[]{:S(2)}, u32[]{:S(2)}) collective-permute-start(f32[4,3,480]{2,1,0:T(4,128)S(1)} %gather_fusion.15), channel_id=1, source_target_pairs={{0,30},{1,31},{2,0},{3,1},{4,2},{5,3},{6,4},{7,5},{8,6},{9,7},{10,... | collective-permute-start | bytes 69128 | tf_op jit(solution)/shard_map/ppermute | solution.py:19
  141.8 4.3 %collective-permute-start.22 = (f32[4,3,480]{2,1,0:T(4,128)S(1)}, f32[4,3,480]{2,1,0:T(4,128)S(1)}, u32[]{:S(2)}, u32[]{:S(2)}) collective-permute-start(f32[4,3,480]{2,1,0:T(4,128)S(1)} %gather_fusion.16), channel_id=1, source_target_pairs={{0,29},{1,30},{2,31},{3,0},{4,1},{5,2},{6,3},{7,4},{8,5},{9,6},{10... | collective-permute-start | bytes 69128 | tf_op jit(solution)/shard_map/ppermute | solution.py:19
  143.3 4.3 %collective-permute-start.23 = (f32[4,3,480]{2,1,0:T(4,128)S(1)}, f32[4,3,480]{2,1,0:T(4,128)S(1)}, u32[]{:S(2)}, u32[]{:S(2)}) collective-permute-start(f32[4,3,480]{2,1,0:T(4,128)S(1)} %gather_fusion.17), channel_id=1, source_target_pairs={{0,28},{1,29},{2,30},{3,31},{4,0},{5,1},{6,2},{7,3},{8,4},{9,5},{1... | collective-permute-start | bytes 69128 | tf_op jit(solution)/shard_map/ppermute | solution.py:19
  (1 other events, 0.7 us)
where the time goes:
time: 234 us; the launch traced here: 232 us
  local copies, waits for them, and re-layouts  92.1 us (39%)
  matrix products  53.4 us (23%)
  other arithmetic  44.2 us (19%)
  starting transfers between devices  37.9 us (16%)
  waiting for transfers between devices  2.95 us (1%)
    dot_general x4, matrix products, per_block(): jnp.einsum('elts,eltsq->eltq', matrices, gathered, precision=lax.Precisio...  53.4 us
    reshape x4, local copies, waits for them, and re-layouts, per_block(): flat_rows[row_index].reshape(block_rows, LEV, NODES, NODES, TRACERS)  43.4 us
    reduce_min x4, other arithmetic, per_block(): lowest = jnp.min(gathered, axis=3)  40.6 us
    ppermute x24, starting transfers between devices, passed_along(): return lax.ppermute(value, axis, pairs)  37.9 us
    gather x4, local copies, waits for them, and re-layouts, per_block(): flat_rows[row_index].reshape(block_rows, LEV, NODES, NODES, TRACERS)  19.9 us
    gather x16, local copies, waits for them, and re-layouts, on_device(): current[asked_lists[slot]]  17.5 us
  transfers between devices with their start and end apart: 24, of which 2 were waited for; matrix products, arithmetic and copies ran while one was open for 9% of the time, Pallas kernels for 0%

commit v1 on v0

v1 whole, which is shorter than its diff:
```python
import functools

import jax
import jax.numpy as jnp
from jax import lax
from jax.experimental import pallas as pl
from jax.experimental.pallas import tpu as pltpu
from jax.sharding import PartitionSpec as P

NODES = 16
TRACERS = 30
PADDED = 32
MESH = pl.DeviceIdType.MESH
F32 = jnp.float32
BF16 = jnp.bfloat16


def high_part(value):
    return value.astype(BF16).astype(F32)


def transposed_dot(a, b):
    return lax.dot_general(a, b, (((1,), (1,)), ((), ())), preferred_element_type=F32)


def kernel(
    tracers, weights, departure, needs, counts, out,
    table, picks, mats, slot_ids, wish, asked, rows, sent, got,
    wish_send, wish_got, row_send, row_got,
):
    count = lax.axis_size("sfc")
    me = lax.axis_index("sfc")
    substeps, elements, levels, _ = weights.shape
    sides, cap = asked.shape[0], asked.shape[1]
    reach = sides // 2
    offsets = [j - reach if j < reach else j - reach + 1 for j in range(sides)]
    wide = NODES * PADDED
    narrow = NODES * TRACERS
    remote = sides * cap
    half = NODES // 2

    barrier = pltpu.get_barrier_semaphore()
    for o in offsets:
        pl.semaphore_signal(barrier, inc=1, device_id=(lax.rem(me + o + count, count),), device_id_type=MESH)

    for j in range(sides):
        for c in range(cap):
            wish[j, c : c + 1, :] = jnp.full((1, 128), needs[0, j, c], jnp.int32)

    pl.semaphore_wait(barrier, sides)

    wishes = []
    for j, o in enumerate(offsets):
        copy = pltpu.make_async_remote_copy(
            src_ref=wish.at[j], dst_ref=asked.at[j],
            send_sem=wish_send.at[j], recv_sem=wish_got.at[j],
            device_id=(lax.rem(me + o + count, count),), device_id_type=MESH,
        )
        copy.start()
        wishes.append(copy)

    spread_row = lax.broadcasted_iota(jnp.int32, (wide, narrow), 0)
    spread_col = lax.broadcasted_iota(jnp.int32, (wide, narrow), 1)
    node, tracer = spread_row // PADDED, spread_row % PADDED
    spread = jnp.where((tracer < TRACERS) & (spread_col == node * TRACERS + tracer), 1.0, 0.0).astype(BF16)
    same = jnp.where(
        lax.broadcasted_iota(jnp.int32, (wide, wide), 0) == lax.broadcasted_iota(jnp.int32, (wide, wide), 1), 1.0, 0.0
    ).astype(BF16)

    for l in range(levels):
        own = tracers[:, l, :]
        high = high_part(own)
        parts = jnp.concatenate([high, own - high], axis=0).astype(BF16)
        table[l, :, 0 : 2 * elements] = transposed_dot(spread, parts).astype(BF16)

    def send_rows(s, l):
        lane = lax.broadcasted_iota(jnp.int32, (remote, 2 * elements), 1) % elements
        choice = jnp.where(rows_asked[...] == lane, 1.0, 0.0).astype(BF16)
        chosen = transposed_dot(choice, table[l, :, 0 : 2 * elements])
        copies = []
        for j, o in enumerate(offsets):
            sent[s, l, j] = chosen[j * cap : (j + 1) * cap, :]
        for j, o in enumerate(offsets):
            copy = pltpu.make_async_remote_copy(
                src_ref=sent.at[s, l, j], dst_ref=got.at[s, l, j],
                send_sem=row_send.at[s, l, j], recv_sem=row_got.at[s, l, j],
                device_id=(lax.rem(me - o + count, count),), device_id_type=MESH,
            )
            copy.start()
            copies.append(copy)
        return copies

    rows_asked = rows[1]
    for copy in wishes:
        copy.wait_recv()
    for j in range(sides):
        rows_asked[j * cap : (j + 1) * cap, :] = asked[j]
    flying = [[send_rows(0, l) for l in range(levels)], [None] * levels]

    ids = lax.broadcasted_iota(jnp.int32, (2 * elements, 256), 0) % elements
    slot_ids[0 : 2 * elements, :] = ids
    slot_ids[2 * elements :, :] = jnp.full((256 - 2 * elements, 256), -1, jnp.int32)
    for j in range(sides):
        for c in range(cap):
            slot = j * cap + c
            live = jnp.where(c < counts[0, j], elements + slot, -1)
            line = jnp.full((1, 256), live, jnp.int32)
            for part in range(2):
                at = 2 * elements + part * remote + slot
                slot_ids[at : at + 1, :] = line

    wanted = jnp.transpose(
        jnp.concatenate([departure[...], jnp.zeros((elements, 128 - levels * NODES), jnp.int32)], axis=1).astype(F32)
    ).astype(jnp.int32)
    for l in range(levels):
        first = wanted[l * NODES : l * NODES + half, :]
        second = wanted[l * NODES + half : (l + 1) * NODES, :]
        both = jnp.concatenate([first, second], axis=1)
        for q in range(half // 2):
            target = jnp.concatenate([both[2 * q : 2 * q + 1, :], both[2 * q + 1 : 2 * q + 2, :]], axis=1)
            picks[l, q] = jnp.where(slot_ids[...] == target, 1.0, 0.0).astype(BF16)
        for s in range(substeps):
            matrix = weights[s, :, l, :]
            mats[s, l] = jnp.transpose(jnp.concatenate([matrix[:, : half * NODES], matrix[:, half * NODES :]], axis=0))

    lane = lax.broadcasted_iota(jnp.int32, (PADDED, 2 * elements), 1)
    left = lane < elements

    for s in range(substeps):
        for l in range(levels):
            for copy in flying[s][l]:
                copy.wait_recv()
            for j in range(sides):
                rows[0][j * cap : (j + 1) * cap, :] = got[s, l, j]
            fetched = rows[0][...]
            high = high_part(fetched)
            low = fetched - high
            parts = jnp.concatenate([high, low, high, low], axis=0).astype(BF16)
            table[l, :, 2 * elements :] = transposed_dot(same, parts).astype(BF16)

            fresh = []
            for q in range(half // 2):
                gathered = jnp.dot(table[l], picks[l, q], preferred_element_type=F32)
                for side in range(2):
                    c = 2 * q + side
                    value = lowest = highest = None
                    for k in range(NODES):
                        item = gathered[k * PADDED : (k + 1) * PADDED, side * 128 : (side + 1) * 128]
                        term = mats[s, l, c * NODES + k : c * NODES + k + 1, :] * item
                        value = term if k == 0 else value + term
                        lowest = item if k == 0 else jnp.minimum(lowest, item)
                        highest = item if k == 0 else jnp.maximum(highest, item)
                    value = jnp.clip(value, lowest, highest)
                    other = pltpu.roll(value, elements, 1)
                    value_high, other_high = high_part(value), high_part(other)
                    fresh.append((c, jnp.where(left, value_high, other - other_high).astype(BF16)))
                    fresh.append((c + half, jnp.where(left, other_high, value - value_high).astype(BF16)))
            for t, block in fresh:
                table[l, t * PADDED : (t + 1) * PADDED, 0 : 2 * elements] = block
            if s + 1 < substeps:
                flying[s + 1][l] = send_rows(s + 1, l)
            else:
                packed = lax.dot_general(
                    table[l, :, 0 : 2 * elements], spread, (((0,), (0,)), ((), ())), preferred_element_type=F32
                )
                out[l] = packed[:elements, :] + packed[elements:, :]

    for copy in wishes:
        copy.wait_send()
    for per_level in flying:
        for copies in per_level:
            for copy in copies:
                copy.wait_send()


def on_device(tracers, weights, departure, needs, counts):
    substeps, elements, levels, _ = weights.shape
    sides, cap = needs.shape[1:]
    wide = NODES * PADDED
    vmem = pl.BlockSpec(memory_space=pltpu.VMEM)
    smem = pl.BlockSpec(memory_space=pltpu.SMEM)
    result = pl.pallas_call(
        kernel,
        out_shape=jax.ShapeDtypeStruct((levels, elements, NODES * TRACERS), F32),
        in_specs=[vmem, vmem, vmem, smem, smem],
        out_specs=vmem,
        scratch_shapes=[
            pltpu.VMEM((levels, wide, 256), BF16),
            pltpu.VMEM((levels, NODES * elements // 256, 256, 256), BF16),
            pltpu.VMEM((substeps, levels, NODES * NODES // 2, 2 * elements), F32),
            pltpu.VMEM((256, 256), jnp.int32),
            pltpu.VMEM((sides, cap, 128), jnp.int32),
            pltpu.VMEM((sides, cap, 128), jnp.int32),
            [pltpu.VMEM((sides * cap, wide), F32), pltpu.VMEM((sides * cap, 128), jnp.int32)],
            pltpu.VMEM((substeps, levels, sides, cap, wide), F32),
            pltpu.VMEM((substeps, levels, sides, cap, wide), F32),
            pltpu.SemaphoreType.DMA((sides,)),
            pltpu.SemaphoreType.DMA((sides,)),
            pltpu.SemaphoreType.DMA((substeps, levels, sides)),
            pltpu.SemaphoreType.DMA((substeps, levels, sides)),
        ],
        compiler_params=pltpu.CompilerParams(collective_id=0, has_side_effects=True, vmem_limit_bytes=60 << 20),
    )(tracers, weights, departure, needs, counts)
    return jnp.transpose(result, (1, 0, 2))


def solution(mesh):
    return jax.shard_map(
        on_device,
        mesh=mesh,
        in_specs=(
            P("sfc", None, None),
            P(None, "sfc", None, None),
            P("sfc", None),
            P("sfc", None, None),
            P("sfc", None),
        ),
        out_specs=P("sfc", None, None),
        check_vma=False,
    )
```

time: 234 us -> 35.1 us (0.15)
  local copies, waits for them, and re-layouts: 92.1 us -> 7.73 us
  matrix products: 53.4 us -> 0 us
  other arithmetic: 44.2 us -> 0 us
  starting transfers between devices: 37.9 us -> 0 us
  Pallas kernels: 0 us -> 27.1 us
  waiting for transfers between devices: 2.95 us -> 0 us
    dot_general x4 -> x0, matrix products: 53.4 us -> none  [per_block(): jnp.einsum('elts,eltsq->eltq', matrices, gathered, precision=lax.Precisio...]
    reshape x11 -> x0, local copies, waits for them, and re-layouts: 46.6 us -> none  [the longest x4 43.4 us: per_block(): flat_rows[row_index].reshape(block_rows, LEV, NODES, NODES, TRACERS)]
    reduce_min x4 -> x0, other arithmetic: 40.6 us -> none  [per_block(): lowest = jnp.min(gathered, axis=3)]
    ppermute x24 -> x0, starting transfers between devices: 37.9 us -> none  [passed_along(): return lax.ppermute(value, axis, pairs)]
    gather x20 -> x0, local copies, waits for them, and re-layouts: 37.4 us -> none  [the longest x4 19.9 us: per_block(): flat_rows[row_index].reshape(block_rows, LEV, NODES, NODES, TRACERS)]
    pallas_call x0 -> x1, Pallas kernels: none -> 27.1 us  [on_device(): pl.pallas_call(kernel, out_shape=jax.ShapeDtypeStruct((levels, elements,...]
    unnamed x16 -> x7, local copies, waits for them, and re-layouts: 0.89 us -> 7.73 us
    ppermute x24 -> x0, waiting for transfers between devices: 2.95 us -> none  [passed_along(): return lax.ppermute(value, axis, pairs)]
  transfers between devices with their start and end apart: 24 -> 0, of which waited for: 2 -> 0; matrix products, arithmetic and copies ran while one was open for 9% -> 0% of each run, Pallas kernels for 0% -> 0%
where the time goes in v1:
time: 35.1 us; the launch traced here: 34.8 us
  Pallas kernels  27.1 us (77%)
  local copies, waits for them, and re-layouts  7.73 us (22%)
    pallas_call x1, Pallas kernels, on_device(): pl.pallas_call(kernel, out_shape=jax.ShapeDtypeStruct((levels, elements,...  27.1 us
    unnamed x7, local copies, waits for them, and re-layouts  7.73 us

profile of v1, /device:TPU:0, one launch (start us, length us, event | category | flops | bytes accessed | tf_op | source)
XLA Modules:
  0.0 34.8 jit_solution(949137886700130542)
XLA Ops:
  0.0 1.3 %copy.9.needs = s32[1,8,4]{2,1,0:T(8,128)} copy(s32[1,8,4]{1,2,0:T(4,128)} %param.8) | data formatting | bytes 256 | tf_op args[3]
  1.3 1.4 %copy.8.departure = s32[64,48]{1,0:T(8,128)} copy(s32[64,48]{0,1:T(8,128)} %param.7) | data formatting | bytes 24576 | tf_op args[2]
  2.8 0.0 copy-start
  2.8 2.1 %copy.6.tracers = f32[64,3,480]{2,1,0:T(4,128)} copy(f32[64,3,480]{2,0,1:T(8,128)} %param.5) | data formatting | bytes 737280 | tf_op args[0]
  4.9 0.0 copy-done
  4.9 1.1 %copy.7.weights = f32[2,64,3,256]{3,2,1,0:T(4,128)} copy(f32[2,64,3,256]{3,1,2,0:T(8,128)S(1)} %copy-done) | data formatting | bytes 786432 | tf_op args[1]
  6.0 27.1 %shard_map.55 = f32[3,64,480]{2,1,0:T(8,128)} custom-call(f32[64,3,480]{2,1,0:T(4,128)} %copy.6.tracers, f32[2,64,3,256]{3,2,1,0:T(4,128)} %copy.7.weights, s32[64,48]{1,0:T(8,128)} %copy.8.departure, s32[1,8,4]{2,1,0:T(8,128)} %copy.9.needs, s32[1,8]{1,0:T(1,128)} %counts.1), custom_call_target="tpu_custom_call" | custom-call | tf_op jit(solution)/shard_map/pallas_call | solution.py:182
  33.1 1.8 %copy.11 = f32[64,3,480]{2,0,1:T(8,128)} copy(f32[64,3,480]{2,0,1:T(8,128)} %bitcast.1) | data formatting | bytes 737280
Async XLA Ops:
  2.8 2.1 %copy-start = (f32[2,64,3,256]{3,1,2,0:T(8,128)S(1)}, f32[2,64,3,256]{3,1,2,0:T(8,128)}, u32[]{:S(2)}) copy-start(f32[2,64,3,256]{3,1,2,0:T(8,128)} %param.6) | copy-start | bytes 1179652

commit v2 on v1

--- a/solution.py
+++ b/solution.py
@@ -30,7 +30,7 @@
 ):
     count = lax.axis_size("sfc")
     me = lax.axis_index("sfc")
-    substeps, elements, levels, _ = weights.shape
+    substeps, levels, elements, _ = weights.shape
     sides, cap = asked.shape[0], asked.shape[1]
     reach = sides // 2
     offsets = [j - reach if j < reach else j - reach + 1 for j in range(sides)]
@@ -45,7 +45,7 @@
 
     for j in range(sides):
         for c in range(cap):
-            wish[j, c : c + 1, :] = jnp.full((1, 128), needs[0, j, c], jnp.int32)
+            wish[j, c : c + 1, :] = jnp.full((1, 128), needs[0, c, j], jnp.int32)
 
     pl.semaphore_wait(barrier, sides)
 
@@ -68,7 +68,7 @@
     ).astype(BF16)
 
     for l in range(levels):
-        own = tracers[:, l, :]
+        own = tracers[l]
         high = high_part(own)
         parts = jnp.concatenate([high, own - high], axis=0).astype(BF16)
         table[l, :, 0 : 2 * elements] = transposed_dot(spread, parts).astype(BF16)
@@ -109,18 +109,15 @@
                 at = 2 * elements + part * remote + slot
                 slot_ids[at : at + 1, :] = line
 
-    wanted = jnp.transpose(
-        jnp.concatenate([departure[...], jnp.zeros((elements, 128 - levels * NODES), jnp.int32)], axis=1).astype(F32)
-    ).astype(jnp.int32)
     for l in range(levels):
-        first = wanted[l * NODES : l * NODES + half, :]
-        second = wanted[l * NODES + half : (l + 1) * NODES, :]
+        first = departure[l * NODES : l * NODES + half, :]
+        second = departure[l * NODES + half : (l + 1) * NODES, :]
         both = jnp.concatenate([first, second], axis=1)
         for q in range(half // 2):
             target = jnp.concatenate([both[2 * q : 2 * q + 1, :], both[2 * q + 1 : 2 * q + 2, :]], axis=1)
             picks[l, q] = jnp.where(slot_ids[...] == target, 1.0, 0.0).astype(BF16)
         for s in range(substeps):
-            matrix = weights[s, :, l, :]
+            matrix = weights[s, l]
             mats[s, l] = jnp.transpose(jnp.concatenate([matrix[:, : half * NODES], matrix[:, half * NODES :]], axis=0))
 
     lane = lax.broadcasted_iota(jnp.int32, (PADDED, 2 * elements), 1)
@@ -200,7 +197,13 @@
             pltpu.SemaphoreType.DMA((substeps, levels, sides)),
         ],
         compiler_params=pltpu.CompilerParams(collective_id=0, has_side_effects=True, vmem_limit_bytes=60 << 20),
-    )(tracers, weights, departure, needs, counts)
+    )(
+        jnp.transpose(tracers, (1, 0, 2)),
+        jnp.transpose(weights, (0, 2, 1, 3)),
+        jnp.transpose(departure),
+        jnp.transpose(needs, (0, 2, 1)),
+        counts,
+    )
     return jnp.transpose(result, (1, 0, 2))
 
 

time: 35.1 us -> 29 us (0.83)
  local copies, waits for them, and re-layouts: 7.73 us -> 1.77 us
    unnamed x7 -> x1, local copies, waits for them, and re-layouts: 7.73 us -> 1.77 us
where the time goes in v2:
time: 29 us; the launch traced here: 28.8 us
  Pallas kernels  27 us (93%)
  local copies, waits for them, and re-layouts  1.77 us (6%)
    pallas_call x1, Pallas kernels, on_device(): pl.pallas_call(kernel, out_shape=jax.ShapeDtypeStruct((levels, elements,...  27 us
    unnamed x1, local copies, waits for them, and re-layouts  1.77 us

profile of v2, /device:TPU:0, one launch (start us, length us, event | category | flops | bytes accessed | tf_op | source)
XLA Modules:
  0.0 28.8 jit_solution(14034188881637002962)
XLA Ops:
  0.0 27.0 %shard_map.55 = f32[3,64,480]{2,1,0:T(8,128)} custom-call(f32[3,64,480]{2,1,0:T(8,128)} %bitcast.6, f32[2,3,64,256]{3,2,1,0:T(8,128)} %bitcast.7, s32[48,64]{1,0:T(8,128)} %bitcast.8, s32[1,4,8]{2,1,0:T(4,128)} %bitcast.9, s32[1,8]{1,0:T(1,128)} %counts.1), custom_call_target="tpu_custom_call" | custom-call | tf_op jit(solution)/shard_map/pallas_call | solution.py:179
  27.0 1.8 %copy.7 = f32[64,3,480]{2,0,1:T(8,128)} copy(f32[64,3,480]{2,0,1:T(8,128)} %bitcast.5) | data formatting | bytes 737280

commit v3 on v2

v3 whole, which is shorter than its diff:
```python
import functools

import jax
import jax.numpy as jnp
from jax import lax
from jax.experimental import pallas as pl
from jax.experimental.pallas import tpu as pltpu
from jax.sharding import PartitionSpec as P

NODES = 16
TRACERS = 30
PADDED = 32
MESH = pl.DeviceIdType.MESH
F32 = jnp.float32
BF16 = jnp.bfloat16


def high_part(value):
    return value.astype(BF16).astype(F32)


def transposed_dot(a, b):
    return lax.dot_general(a, b, (((1,), (1,)), ((), ())), preferred_element_type=F32)


def kernel(
    tracers_far, weights_far, departure_far, needs, counts, out_far,
    tracers, weights, departure, out, table, picks, mats, slot_ids, wish, asked, rows, rows_asked, sent, got,
    spread, same, wish_send, wish_got, row_send, row_got, loaded, stored,
):
    count = lax.axis_size("sfc")
    me = lax.axis_index("sfc")
    substeps, levels, elements, _ = weights.shape
    sides, cap = asked.shape[0], asked.shape[1]
    reach = sides // 2
    offsets = [j - reach if j < reach else j - reach + 1 for j in range(sides)]
    wide = NODES * PADDED
    narrow = NODES * TRACERS
    remote = sides * cap
    half = NODES // 2
    own_lanes = 2 * elements

    def device(offset):
        return (lax.rem(me + offset + count, count),)

    barrier = pltpu.get_barrier_semaphore()
    for o in offsets:
        pl.semaphore_signal(barrier, inc=1, device_id=device(o), device_id_type=MESH)

    loads = [
        pltpu.make_async_copy(far, near, loaded.at[i])
        for i, (far, near) in enumerate(((tracers_far, tracers), (departure_far, departure), (weights_far, weights)))
    ]
    for load in loads:
        load.start()

    for j in range(sides):
        for c in range(cap):
            wish[j, c : c + 1, :] = jnp.full((1, 128), needs[0, c, j], jnp.int32)

    pl.semaphore_wait(barrier, sides)

    wishes = []
    for j, o in enumerate(offsets):
        copy = pltpu.make_async_remote_copy(
            src_ref=wish.at[j], dst_ref=asked.at[j],
            send_sem=wish_send.at[j], recv_sem=wish_got.at[j],
            device_id=device(o), device_id_type=MESH,
        )
        copy.start()
        wishes.append(copy)

    def row_copy(s, l, j):
        return pltpu.make_async_remote_copy(
            src_ref=sent.at[s, l, j], dst_ref=got.at[s, l, j],
            send_sem=row_send.at[s, l, j], recv_sem=row_got.at[s, l, j],
            device_id=device(-offsets[j]), device_id_type=MESH,
        )

    def build_spread(k, _):
        tracer = lax.broadcasted_iota(jnp.int32, (PADDED, narrow), 0)
        column = lax.broadcasted_iota(jnp.int32, (PADDED, narrow), 1) - k * TRACERS
        column = jnp.where(tracer < TRACERS, column, -1)
        spread[pl.ds(pl.multiple_of(k * PADDED, PADDED), PADDED), :] = jnp.where(column == tracer, 1.0, 0.0).astype(BF16)
        return 0

    lax.fori_loop(0, NODES, build_spread, 0)
    same[...] = jnp.where(
        lax.broadcasted_iota(jnp.int32, (128, 128), 0) == lax.broadcasted_iota(jnp.int32, (128, 128), 1), 1.0, 0.0
    ).astype(BF16)

    loads[0].wait()

    def build_table(l, _):
        own = tracers[l]
        high = high_part(own)
        parts = jnp.concatenate([high, own - high], axis=0).astype(BF16)
        table[0, l, :, 0:own_lanes] = transposed_dot(spread[...], parts).astype(BF16)
        return 0

    for l in range(levels):
        build_table(l, 0)

    def send_rows(s, l):
        lane = lax.broadcasted_iota(jnp.int32, (remote, own_lanes), 1) % elements
        choice = jnp.where(rows_asked[...] == lane, 1.0, 0.0).astype(BF16)
        chosen = transposed_dot(choice, table[s, l, :, 0:own_lanes])
        for j in range(sides):
            sent[s, l, j] = chosen[j * cap : (j + 1) * cap, :]
        for j in range(sides):
            row_copy(s, l, j).start()

    for copy in wishes:
        copy.wait_recv()
    for j in range(sides):
        rows_asked[j * cap : (j + 1) * cap, :] = asked[j]

    def first_rows(l, _):
        send_rows(0, l)
        return 0

    for l in range(levels):
        first_rows(l, 0)

    slot_ids[0:own_lanes, :] = lax.broadcasted_iota(jnp.int32, (own_lanes, 256), 0) % elements
    slot_ids[own_lanes:, :] = jnp.full((256 - own_lanes, 256), -1, jnp.int32)
    for j in range(sides):
        for c in range(cap):
            slot = j * cap + c
            live = jnp.where(c < counts[0, j], elements + slot, -1)
            line = jnp.full((1, 256), live, jnp.int32)
            for part in range(2):
                at = own_lanes + part * remote + slot
                slot_ids[at : at + 1, :] = line

    loads[1].wait()
    loads[2].wait()

    def build_picks(l, _):
        base = l * NODES
        first = departure[pl.ds(base, half), :]
        second = departure[pl.ds(base + half, half), :]
        both = jnp.concatenate([first, second], axis=1)
        for q in range(half // 2):
            target = jnp.concatenate([both[2 * q : 2 * q + 1, :], both[2 * q + 1 : 2 * q + 2, :]], axis=1)
            picks[l, q] = jnp.where(slot_ids[...] == target, 1.0, 0.0).astype(BF16)
        for s in range(substeps):
            matrix = weights[s, l]
            mats[s, l] = jnp.transpose(jnp.concatenate([matrix[:, : half * NODES], matrix[:, half * NODES :]], axis=0))
        return 0

    for l in range(levels):
        build_picks(l, 0)

    left = lax.broadcasted_iota(jnp.int32, (PADDED, own_lanes), 1) < elements

    def one_level(turn, _):
        s, l = turn // levels, turn % levels
        for j in range(sides):
            row_copy(s, l, j).wait_recv()
        for j in range(sides):
            rows[j * cap : (j + 1) * cap, :] = got[s, l, j]
        fetched = rows[...]
        high = high_part(fetched)
        low = fetched - high
        parts = jnp.concatenate([high, low, high, low], axis=0).astype(BF16)
        for at in range(0, wide, 128):
            table[s, l, at : at + 128, own_lanes:] = transposed_dot(same[...], parts[:, at : at + 128]).astype(BF16)

        def one_pair(q, _):
            gathered = jnp.dot(table[s, l], picks[l, q], preferred_element_type=F32)
            for side in range(2):
                c = 2 * q + side
                matrix = mats[s, l, pl.ds(c * NODES, NODES), :]
                value = lowest = highest = None
                for k in range(NODES):
                    item = gathered[k * PADDED : (k + 1) * PADDED, side * 128 : (side + 1) * 128]
                    term = matrix[k : k + 1, :] * item
                    value = term if k == 0 else value + term
                    lowest = item if k == 0 else jnp.minimum(lowest, item)
                    highest = item if k == 0 else jnp.maximum(highest, item)
                value = jnp.clip(value, lowest, highest)
                other = pltpu.roll(value, elements, 1)
                value_high, other_high = high_part(value), high_part(other)
                near = c * PADDED
                past = (c + half) * PADDED
                table[s + 1, l, pl.ds(near, PADDED), 0:own_lanes] = jnp.where(left, value_high, other - other_high).astype(BF16)
                table[s + 1, l, pl.ds(past, PADDED), 0:own_lanes] = jnp.where(left, other_high, value - value_high).astype(BF16)
            return 0

        for q in range(half // 2):
            one_pair(q, 0)

        if s + 1 < substeps:
            send_rows(s + 1, l)

        else:
            packed = lax.dot_general(
                table[s + 1, l, :, 0:own_lanes], spread[...], (((0,), (0,)), ((), ())), preferred_element_type=F32
            )
            out[l] = packed[:elements, :] + packed[elements:, :]
            pltpu.make_async_copy(out.at[l], out_far.at[l], stored.at[l]).start()

        return 0

    for turn in range(substeps * levels):
        one_level(turn, 0)

    for copy in wishes:
        copy.wait_send()
    for s in range(substeps):
        for l in range(levels):
            for j in range(sides):
                row_copy(s, l, j).wait_send()
    for l in range(levels):
        pltpu.make_async_copy(out.at[l], out_far.at[l], stored.at[l]).wait()


def on_device(tracers, weights, departure, needs, counts):
    substeps, elements, levels, _ = weights.shape
    sides, cap = needs.shape[1:]
    wide = NODES * PADDED
    far = pl.BlockSpec(memory_space=pl.ANY)
    smem = pl.BlockSpec(memory_space=pltpu.SMEM)
    result = pl.pallas_call(
        kernel,
        out_shape=jax.ShapeDtypeStruct((levels, elements, NODES * TRACERS), F32),
        in_specs=[far, far, far, smem, smem],
        out_specs=far,
        scratch_shapes=[
            pltpu.VMEM((levels, elements, NODES * TRACERS), F32),
            pltpu.VMEM((substeps, levels, elements, NODES * NODES), F32),
            pltpu.VMEM((levels * NODES, elements), jnp.int32),
            pltpu.VMEM((levels, elements, NODES * TRACERS), F32),
            pltpu.VMEM((substeps + 1, levels, wide, 256), BF16),
            pltpu.VMEM((levels, NODES * elements // 256, 256, 256), BF16),
            pltpu.VMEM((substeps, levels, NODES * NODES // 2, 2 * elements), F32),
            pltpu.VMEM((256, 256), jnp.int32),
            pltpu.VMEM((sides, cap, 128), jnp.int32),
            pltpu.VMEM((sides, cap, 128), jnp.int32),
            pltpu.VMEM((sides * cap, wide), F32),
            pltpu.VMEM((sides * cap, 128), jnp.int32),
            pltpu.VMEM((substeps, levels, sides, cap, wide), F32),
            pltpu.VMEM((substeps, levels, sides, cap, wide), F32),
            pltpu.VMEM((wide, NODES * TRACERS), BF16),
            pltpu.VMEM((128, 128), BF16),
            pltpu.SemaphoreType.DMA((sides,)),
            pltpu.SemaphoreType.DMA((sides,)),
            pltpu.SemaphoreType.DMA((substeps, levels, sides)),
            pltpu.SemaphoreType.DMA((substeps, levels, sides)),
            pltpu.SemaphoreType.DMA((3,)),
            pltpu.SemaphoreType.DMA((levels,)),
        ],
        compiler_params=pltpu.CompilerParams(collective_id=0, has_side_effects=True, vmem_limit_bytes=60 << 20),
    )(
        jnp.transpose(tracers, (1, 0, 2)),
        jnp.transpose(weights, (0, 2, 1, 3)),
        jnp.transpose(departure),
        jnp.transpose(needs, (0, 2, 1)),
        counts,
    )
    return jnp.transpose(result, (1, 0, 2))


def solution(mesh):
    return jax.shard_map(
        on_device,
        mesh=mesh,
        in_specs=(
            P("sfc", None, None),
            P(None, "sfc", None, None),
            P("sfc", None),
            P("sfc", None, None),
            P("sfc", None),
        ),
        out_specs=P("sfc", None, None),
        check_vma=False,
    )
```

time: 29 us -> 27.7 us (0.955)
  Pallas kernels: 27 us -> 25.7 us
    pallas_call x1, Pallas kernels: 27 us -> 25.7 us  [on_device(): pl.pallas_call(kernel, out_shape=jax.ShapeDtypeStruct((levels, elements,...]
where the time goes in v3:
time: 27.7 us; the launch traced here: 27.5 us
  Pallas kernels  25.7 us (93%)
  local copies, waits for them, and re-layouts  1.77 us (6%)
    pallas_call x1, Pallas kernels, on_device(): pl.pallas_call(kernel, out_shape=jax.ShapeDtypeStruct((levels, elements,...  25.7 us
    unnamed x1, local copies, waits for them, and re-layouts  1.77 us

profile of v3, /device:TPU:0, one launch (start us, length us, event | category | flops | bytes accessed | tf_op | source)
XLA Modules:
  0.0 27.5 jit_solution(5091094514572574874)
XLA Ops:
  0.0 25.7 %shard_map.55 = f32[3,64,480]{2,1,0:T(8,128)} custom-call(f32[3,64,480]{2,1,0:T(8,128)} %bitcast.6, f32[2,3,64,256]{3,2,1,0:T(8,128)} %bitcast.7, s32[48,64]{1,0:T(8,128)} %bitcast.8, s32[1,4,8]{2,1,0:T(4,128)} %bitcast.9, s32[1,8]{1,0:T(1,128)} %counts.1), custom_call_target="tpu_custom_call" | custom-call | tf_op jit(solution)/shard_map/pallas_call | solution.py:225
  25.7 1.8 %copy.7 = f32[64,3,480]{2,0,1:T(8,128)} copy(f32[64,3,480]{2,0,1:T(8,128)} %bitcast.5) | data formatting | bytes 737280
